TPU v7x, 32 devices: a whole 2x2x4 slice. The times are simulated.
32 devices in a mesh: re: 4 (over y, x), ka: 8 (over z, core).
Axes of the slice: x: 2, y: 2, z: 4, core: 2. Of those that a mesh axis runs over, the one named last changes fastest.
Arguments:
- lattice_blocks: bfloat16 [192, 2, 3, 256], P(('re', 'ka')), may hold values from -0.4375 to 0.4375
- lattice_coords: int32 [192, 3], P(('re', 'ka')), may hold values from -8 to 8
- kpoint_index: int32 [192, 3], P('ka'), may hold values from 0 to 63
- polarization: float32 [3], replicated, may hold values from -4 to 4
- energy_gap: float32 [192, 32], P('ka'), may hold values from 0.5 to 2.5
- coupling: bfloat16 [8, 96, 2, 32, 8], P('ka', 're'), may hold values from -1 to 1
- phonon_weight: bfloat16 [8, 96], P('ka', 're'), may hold values from 0.19921875 to 5
Outputs:
- rates: float32 [192, 8], P('ka', 're')
All inputs are finite; a program needn't handle non-finite values.
Results may differ from a plain program's by a relative error of at most 0.0014.
Values may be sent and summed in bfloat16 or wider, within the bound.
A program may use at most 128 MiB of HBM per device.

v0:
```python
import math
import jax
import jax.numpy as jnp
from jax import lax
from jax.sharding import PartitionSpec as P

NV = 8
NC = 8
NMODE = 96
NKG = 64


def phase_rows(kpoint_index, coords):
    turns = jnp.mod(jnp.sum(kpoint_index[:, None, :] * coords[None, :, :], axis=2), NKG)
    angle = turns.astype(jnp.float32) * (2.0 * math.pi / NKG)
    cosine = jnp.cos(angle).astype(jnp.bfloat16)
    sine = jnp.sin(angle).astype(jnp.bfloat16)
    count = kpoint_index.shape[0]
    upper = jnp.stack([cosine, -sine], axis=2).reshape(count, -1)
    lower = jnp.stack([sine, cosine], axis=2).reshape(count, -1)
    return jnp.concatenate([upper, lower], axis=0)


def left_factor(momenta, polarization, energy_gap):
    count = momenta.shape[1]
    parts = momenta.reshape(2, count, 3, NV, -1)
    along = (
        parts[:, :, 0] * polarization[0]
        + parts[:, :, 1] * polarization[1]
        + parts[:, :, 2] * polarization[2]
    )
    return (along / energy_gap[None, :, None, :]).astype(jnp.bfloat16).reshape(2, count * NV, -1)


def rate_block(factor, coup, weight):

    def product(left, right):
        return jnp.einsum("qvmj,am->qvja", right, left, preferred_element_type=jnp.float32)

    real_left, imag_left = (factor[0], factor[1])
    real_right, imag_right = (coup[:, :, 0], coup[:, :, 1])
    are = product(real_left, real_right) - product(imag_left, imag_right)
    aim = product(real_left, imag_right) + product(imag_left, real_right)
    power = (are * are + aim * aim) * weight.astype(jnp.float32)[:, :, None, None]
    summed = jnp.sum(power, axis=(1, 2))
    count = factor.shape[1] // NV
    qcount = coup.shape[0]
    return jnp.sum(summed.reshape(qcount, count, NV), axis=2).T * (1.0 / (NMODE * NV * NC))


def body(
    lattice_blocks, lattice_coords, kpoint_index, polarization, energy_gap, coupling, phonon_weight
):
    own_count = kpoint_index.shape[0]
    cols = lattice_blocks.shape[2] * lattice_blocks.shape[3]
    blocks = lax.all_gather(lattice_blocks, "ka", axis=0, tiled=True)
    coords = lax.all_gather(lattice_coords.astype(jnp.bfloat16), "ka", axis=0, tiled=True)
    left = phase_rows(kpoint_index, coords.astype(jnp.int32))
    partial_value = jnp.dot(left, blocks.reshape(-1, cols), preferred_element_type=jnp.float32)
    momenta = lax.psum(partial_value, "re").reshape(2, own_count, cols)
    factor = left_factor(momenta, polarization, energy_gap)
    partial_rates = rate_block(
        factor,
        lax.all_gather(coupling, "ka", axis=0, tiled=True),
        lax.all_gather(phonon_weight, "ka", axis=0, tiled=True),
    )
    return lax.psum_scatter(partial_rates, "re", scatter_dimension=1, tiled=True)


def solution(mesh):
    return jax.shard_map(
        body,
        mesh=mesh,
        in_specs=(
            P(("re", "ka"), None, None, None),
            P(("re", "ka"), None),
            P("ka", None),
            P(),
            P("ka", None),
            P("ka", "re", None, None, None),
            P("ka", "re"),
        ),
        out_specs=P("ka", "re"),
        check_vma=False,
    )
```

profile of v0, /device:TPU:0, one launch (start us, length us, event | category | flops | bytes accessed | tf_op | source)
XLA Modules:
  0.0 103.5 jit_solution(17837021338715821611)
XLA Ops:
  6.5 0.7 convert_bitcast_fusion
  7.2 13.5 %all-gather = bf16[8,6,3]{1,2,0:T(4,128)(2,1)S(1)} all-gather(bf16[1,6,3]{1,2,0:T(4,128)(2,1)S(1)} %convert_bitcast_fusion), channel_id=1, replica_groups=mesh['re'=4,'ka'=8] {'ka'}, dimensions={0}, use_global_device_ids=true | all-gather | bytes 324 | tf_op jit(solution)/shard_map/all_gather | solution.py:57
  20.7 0.1 reshape.103
  20.8 0.8 multiply_reduce_fusion.1
  21.7 0.1 copy.53
  21.8 0.1 copy.54
  21.9 14.2 %all_gather.13 = bf16[48,2,3,256]{3,1,2,0:T(2,128)(2,1)S(1)} all-gather(bf16[6,2,3,256]{3,1,2,0:T(2,128)(2,1)} %param.7), channel_id=1, replica_groups=mesh['re'=4,'ka'=8] {'ka'}, dimensions={0}, use_global_device_ids=true | all-gather | bytes 165888 | tf_op jit(solution)/shard_map/all_gather | solution.py:56
  36.2 0.3 fusion.8
  36.5 0.2 reshape_reshape.3
  36.8 0.8 copy.56
  37.7 16.3 %all_gather.14 = bf16[8,24,2,32,8]{3,1,4,0,2:T(8,128)(2,1)S(1)} all-gather(bf16[1,24,2,32,8]{3,1,4,0,2:T(8,128)(2,1)S(1)} %copy.57), channel_id=1, replica_groups=mesh['re'=4,'ka'=8] {'ka'}, dimensions={0}, use_global_device_ids=true | all-gather | bytes 221184 | tf_op jit(solution)/shard_map/all_gather | solution.py:64
  53.9 8.7 %all-gather.1 = bf16[8,1,24]{2,1,0:T(2,128)(2,1)S(1)} all-gather(bf16[1,1,24]{2,1,0:T(2,128)(2,1)S(1)} %bitcast.62), channel_id=1, replica_groups=mesh['re'=4,'ka'=8] {'ka'}, dimensions={0}, use_global_device_ids=true | all-gather | bytes 432 | tf_op jit(solution)/shard_map/all_gather | solution.py:65
  62.7 0.6 dynamic-slice
  63.9 0.6 fusion.17
  64.6 17.4 %all-reduce.3.cloned.1.call-done = f32[2,24,3,8,32]{4,3,1,0,2:T(8,128)} async-done(((f32[2,24,3,8,32]{4,3,1,0,2:T(8,128)}), f32[2,24,3,8,32]{4,3,1,0,2:T(8,128)}) %all-reduce.3.cloned.1.call-update) | async-done | bytes 147472 | tf_op jit(solution)/shard_map/psum | solution.py:60
  82.0 3.1 %fusion.7 = bf16[2,24,8,32]{3,2,1,0:T(8,128)(2,1)S(1)} fusion(f32[2,24,3,8,32]{4,3,1,0,2:T(8,128)} %all-reduce.3.cloned.1.call-done, f32[24,32]{1,0:T(8,128)S(1)} %copy-done.1, f32[]{:T(128)} %bitcast.6, f32[]{:T(128)} %bitcast.5, f32[]{:T(128)} %bitcast.4), kind=kLoop, calls=%fused_computation.13 | loop fusion | flops 86016 | bytes 175116 | tf_op jit(solution)/shard_map/convert_element_type | solution.py:32
  85.1 0.4 fusion
  85.5 0.4 fusion.2
  85.9 0.4 fusion.1
  86.3 0.7 multiply_reduce_fusion
  87.0 0.1 reshape.98
  87.1 0.1 reduce_sum.35
  87.2 8.9 %all-reduce = f32[24,8]{0,1:T(8,128)S(1)} all-reduce(f32[24,8]{0,1:T(8,128)S(1)} %multiply_bitcast_fusion), channel_id=2, replica_groups=mesh['re'=4,'ka'=8] {'re'}, use_global_device_ids=true, to_apply=%region_4.5.clone | all-reduce | flops 192 | bytes 1536
  96.1 0.6 constant_dynamic-slice_fusion
  (21 shorter events, 0.3 us)
Async XLA Ops:
  6.5 75.5 %all-reduce.3.cloned.1.call-start = ((), (), s32[]{:S(2)}) async-start(), calls=%async_computation | async-start | bytes 1179648 | tf_op jit(solution)/shard_map/psum | solution.py:60
  36.2 1.4 %copy-start = (bf16[1,24,2,32,8]{3,4,2,1,0:T(8,128)(2,1)S(1)}, bf16[1,24,2,32,8]{3,4,2,1,0:T(8,128)(2,1)}, u32[]{:S(2)}) copy-start(bf16[1,24,2,32,8]{3,4,2,1,0:T(8,128)(2,1)} %param.12) | copy-start | bytes 73732
  36.7 17.2 %copy-start.3 = (bf16[1,24]{1,0:T(2,128)(2,1)S(1)}, bf16[1,24]{1,0:T(2,128)(2,1)}, u32[]{:S(2)}) copy-start(bf16[1,24]{1,0:T(2,128)(2,1)} %param.13) | copy-start | bytes 148
  36.7 25.9 %copy-start.4 = (u32[32]{0:T(128)S(1)}, u32[32]{0:T(128)}, u32[]{:S(2)}) copy-start(u32[32]{0:T(128)} %constant.28) | copy-start | bytes 388
  36.7 27.2 %copy-start.2 = (f32[3]{0:T(128)S(1)}, f32[3]{0:T(128)}, u32[]{:S(2)}) copy-start(f32[3]{0:T(128)} %param.10) | copy-start | bytes 40
  36.8 45.3 %copy-start.1 = (f32[24,32]{1,0:T(8,128)S(1)}, f32[24,32]{1,0:T(8,128)}, u32[]{:S(2)}) copy-start(f32[24,32]{1,0:T(8,128)} %param.11) | copy-start | bytes 9220
Sparse Core Ops, SparseCore 0:
  37.8 44.1 all-reduce.2
where the time goes:
time: 104 us
  blocking collectives  61.6 us (59%)
  waiting for transfers between devices  17.5 us (17%)
  between operations  14.2 us (14%)
  other arithmetic  4.75 us (5%)
  local copies, waits for them, and re-layouts  3.38 us (3%)
  matrix products  2.13 us (2%)
    psum x1, waiting for transfers between devices, body(): momenta = lax.psum(partial_value, 're').reshape(2, own_count, cols)  17.4 us
    all_gather x1, blocking collectives, body(): lax.all_gather(coupling, 'ka', axis=0, tiled=True)  16.3 us
    all_gather x1, blocking collectives, body(): blocks = lax.all_gather(lattice_blocks, 'ka', axis=0, tiled=True)  14.2 us
    all_gather x1, blocking collectives, body(): lax.all_gather(lattice_coords.astype(jnp.bfloat16), 'ka', axis=0, tiled=T...  13.5 us
    unnamed x1, blocking collectives  8.93 us
    all_gather x1, blocking collectives, body(): lax.all_gather(phonon_weight, 'ka', axis=0, tiled=True)  8.72 us
    convert_element_type x1, other arithmetic, left_factor(): (along / energy_gap[None, :, None, :]).astype(jnp.bfloat16)  3.05 us
  transfers between devices with their start and end apart: 1, of which 1 were waited for; matrix products, arithmetic and copies ran while one was open for 1% of the time, Pallas kernels for 0%

commit v1 on v0

--- a/solution.py
+++ b/solution.py
@@ -57,7 +57,12 @@
     coords = lax.all_gather(lattice_coords.astype(jnp.bfloat16), "ka", axis=0, tiled=True)
     left = phase_rows(kpoint_index, coords.astype(jnp.int32))
     partial_value = jnp.dot(left, blocks.reshape(-1, cols), preferred_element_type=jnp.float32)
-    momenta = lax.psum(partial_value, "re").reshape(2, own_count, cols)
+
+    def edges_link(field_in, a_name):
+        part_now = jax.lax.all_gather(field_in, a_name)
+        return jnp.sum(part_now, 0)
+
+    momenta = edges_link(partial_value, "re").reshape(2, own_count, cols)
     factor = left_factor(momenta, polarization, energy_gap)
     partial_rates = rate_block(
         factor,

time: 104 us -> 81.4 us (0.78)
  waiting for transfers between devices: 17.5 us -> 0 us
  between operations: 14.2 us -> 0.83 us
  blocking collectives: 61.6 us -> 72 us
  other arithmetic: 4.75 us -> 3.67 us
    psum x1 -> x0, waiting for transfers between devices: 17.4 us -> none  [body(): momenta = lax.psum(partial_value, 're').reshape(2, own_count, cols)]
    all_gather x0 -> x1, blocking collectives: none -> 10.8 us  [edges_link(): part_now = jax.lax.all_gather(field_in, a_name)]
    convert_element_type x1, other arithmetic: 3.05 us -> 1.95 us  [left_factor(): (along / energy_gap[None, :, None, :]).astype(jnp.bfloat16)]
  transfers between devices with their start and end apart: 1 -> 0, of which waited for: 1 -> 0; matrix products, arithmetic and copies ran while one was open for 1% -> 0% of each run, Pallas kernels for 0% -> 0%
where the time goes in v1:
time: 81.4 us; the launch traced here: 81.1 us
  blocking collectives  72 us (88%)
  other arithmetic  3.67 us (5%)
  local copies, waits for them, and re-layouts  2.53 us (3%)
  matrix products  2.12 us (3%)
  between operations  0.83 us (1%)
    all_gather x1, blocking collectives, body(): lax.all_gather(coupling, 'ka', axis=0, tiled=True)  15.7 us
    all_gather x1, blocking collectives, body(): blocks = lax.all_gather(lattice_blocks, 'ka', axis=0, tiled=True)  14.2 us
    all_gather x1, blocking collectives, body(): lax.all_gather(lattice_coords.astype(jnp.bfloat16), 'ka', axis=0, tiled=T...  13.5 us
    all_gather x1, blocking collectives, edges_link(): part_now = jax.lax.all_gather(field_in, a_name)  10.8 us
    unnamed x1, blocking collectives  8.97 us
    all_gather x1, blocking collectives, body(): lax.all_gather(phonon_weight, 'ka', axis=0, tiled=True)  8.77 us
    convert_element_type x1, other arithmetic, left_factor(): (along / energy_gap[None, :, None, :]).astype(jnp.bfloat16)  1.95 us
    dot_general x4, matrix products, product(): jnp.einsum('qvmj,am->qvja', right, left, preferred_element_type=jnp.float32)  1.86 us

profile of v1, /device:TPU:0, one launch (start us, length us, event | category | flops | bytes accessed | tf_op | source)
XLA Modules:
  0.0 81.1 jit_solution(11116556980021993344)
XLA Ops:
  0.0 0.7 convert_bitcast_fusion
  0.7 13.5 %all-gather.1 = bf16[8,6,3]{1,2,0:T(4,128)(2,1)S(1)} all-gather(bf16[1,6,3]{1,2,0:T(4,128)(2,1)S(1)} %convert_bitcast_fusion), channel_id=1, replica_groups=mesh['re'=4,'ka'=8] {'ka'}, dimensions={0}, use_global_device_ids=true | all-gather | bytes 324 | tf_op jit(solution)/shard_map/all_gather | solution.py:57
  14.2 0.1 reshape.104
  14.2 0.8 multiply_reduce_fusion.1
  15.2 0.1 copy.48
  15.3 0.1 copy.49
  15.4 14.2 %all_gather.19 = bf16[48,2,3,256]{3,1,2,0:T(2,128)(2,1)S(1)} all-gather(bf16[6,2,3,256]{3,1,2,0:T(2,128)(2,1)} %param.7), channel_id=1, replica_groups=mesh['re'=4,'ka'=8] {'ka'}, dimensions={0}, use_global_device_ids=true | all-gather | bytes 165888 | tf_op jit(solution)/shard_map/all_gather | solution.py:56
  29.6 0.1 copy.50
  29.7 0.3 fusion.8
  30.0 10.8 %all-gather = f32[192,768]{1,0:T(8,128)S(1)} all-gather(f32[48,768]{1,0:T(8,128)S(1)} %fusion.8), channel_id=2, replica_groups=mesh['re'=4,'ka'=8] {'re'}, dimensions={0}, use_global_device_ids=true | all-gather | bytes 737280 | tf_op jit(solution)/shard_map/all_gather | solution.py:62
  40.8 0.2 reshape_reshape.3
  41.1 0.7 fusion.17
  41.7 1.9 %fusion.7 = bf16[2,24,8,32]{3,2,1,0:T(8,128)(2,1)S(1)} fusion(f32[2,24,3,8,32]{4,3,2,1,0:T(8,128)S(1)} %reshape_reshape.3, f32[24,32]{1,0:T(8,128)S(1)} %copy-done.1, f32[]{:T(128)} %bitcast.7, f32[]{:T(128)} %bitcast.6, f32[]{:T(128)} %bitcast.5), kind=kLoop, calls=%fused_computation.13 | loop fusion | flops 86016 | bytes 175116 | tf_op jit(solution)/shard_map/convert_element_type | solution.py:32
  43.7 15.7 %all_gather.22 = bf16[8,24,2,32,8]{3,1,4,0,2:T(8,128)(2,1)S(1)} all-gather(bf16[1,24,2,32,8]{3,1,4,0,2:T(8,128)(2,1)S(1)} %copy.51), channel_id=1, replica_groups=mesh['re'=4,'ka'=8] {'ka'}, dimensions={0}, use_global_device_ids=true | all-gather | bytes 221184 | tf_op jit(solution)/shard_map/all_gather | solution.py:69
  59.5 0.4 fusion
  59.9 0.4 fusion.2
  60.3 0.4 fusion.1
  60.7 8.8 %all-gather.2 = bf16[8,1,24]{2,1,0:T(2,128)(2,1)S(1)} all-gather(bf16[1,1,24]{2,1,0:T(2,128)(2,1)S(1)} %bitcast.64), channel_id=1, replica_groups=mesh['re'=4,'ka'=8] {'ka'}, dimensions={0}, use_global_device_ids=true | all-gather | bytes 432 | tf_op jit(solution)/shard_map/all_gather | solution.py:70
  69.5 0.7 multiply_reduce_fusion
  70.1 0.1 reshape.98
  70.2 0.1 reduce_sum.45
  70.4 9.0 %all-reduce = f32[24,8]{0,1:T(8,128)S(1)} all-reduce(f32[24,8]{0,1:T(8,128)S(1)} %multiply_bitcast_fusion), channel_id=3, replica_groups=mesh['re'=4,'ka'=8] {'re'}, use_global_device_ids=true, to_apply=%region_4.5.clone | all-reduce | flops 192 | bytes 1536
  79.3 0.6 dynamic-slice
  80.6 0.6 constant_dynamic-slice_fusion
  (19 shorter events, 0.3 us)
Async XLA Ops:
  29.6 11.5 %copy-start.2 = (f32[3]{0:T(128)S(1)}, f32[3]{0:T(128)}, u32[]{:S(2)}) copy-start(f32[3]{0:T(128)} %param.10) | copy-start | bytes 40
  29.6 12.1 %copy-start.1 = (f32[24,32]{1,0:T(8,128)S(1)}, f32[24,32]{1,0:T(8,128)}, u32[]{:S(2)}) copy-start(f32[24,32]{1,0:T(8,128)} %param.11) | copy-start | bytes 9220
  29.7 14.0 %copy-start = (bf16[1,24,2,32,8]{3,4,2,1,0:T(8,128)(2,1)S(1)}, bf16[1,24,2,32,8]{3,4,2,1,0:T(8,128)(2,1)}, u32[]{:S(2)}) copy-start(bf16[1,24,2,32,8]{3,4,2,1,0:T(8,128)(2,1)} %param.12) | copy-start | bytes 73732
  59.9 0.8 %copy-start.3 = (bf16[1,24]{1,0:T(2,128)(2,1)S(1)}, bf16[1,24]{1,0:T(2,128)(2,1)}, u32[]{:S(2)}) copy-start(bf16[1,24]{1,0:T(2,128)(2,1)} %param.13) | copy-start | bytes 148
  69.5 9.9 %copy-start.4 = (u32[32]{0:T(128)S(1)}, u32[32]{0:T(128)}, u32[]{:S(2)}) copy-start(u32[32]{0:T(128)} %constant.28) | copy-start | bytes 388
